TPU v7x, 256 devices: a whole 4x4x8 slice. The times are simulated.
256 devices in a mesh: seq: 32 (over x_lo, z, core), head: 8 (over y, x_hi).
Axes of the slice: x: 4 (x_hi: 2, x_lo: 2; x = x_hi * 2 + x_lo), y: 4, z: 8, core: 2. Of those that a mesh axis runs over, the one named last changes fastest.
Arguments:
- query_rows: bfloat16 [6144, 2048], P('seq', 'head'), may hold values from -6 to 6
- key_rows: bfloat16 [6144, 2048], P('seq', 'head'), may hold values from -6 to 6
- value_rows: bfloat16 [6144, 2048], P('seq', 'head'), may hold values from -6 to 6
- grad_output: bfloat16 [6144, 2048], P('seq', 'head'), may hold values from -6 to 6
- positions: int32 [6144], P('seq'), may hold values from 0 to 6143, each once
Outputs:
- grad_query: bfloat16 [6144, 2048], P(('seq', 'head'))
- grad_keys: bfloat16 [6144, 2048], P('seq', 'head')
- grad_values: bfloat16 [6144, 2048], P('seq', 'head')
Inputs may be any that keep to these rules, and one draw needn't show every extreme that they name: `positions`: each number from 0 to 6143 appears once.
All inputs are finite; a program needn't handle non-finite values.
Results may differ from a plain program's by a relative error of at most 0.012.
Values may be sent and summed in bfloat16 or wider, within the bound.
A program may use at most 128 MiB of HBM per device.

v0:
```python
import jax
import jax.numpy as jnp
from jax import lax
from jax.sharding import PartitionSpec as P

HEAD_DIM = 128


def side_by_side(arrays, axis, dim, along):
    ends, at = ([], 0)
    for a in arrays[:-1]:
        at += a.shape[along]
        ends.append(at)
    both = jnp.concatenate(arrays, axis=along)
    return tuple(jnp.split(lax.all_gather(both, axis, axis=dim, tiled=True), ends, axis=along))


def in_blocks(value, dim, size):
    lengths = value.shape
    parts = value.reshape(*lengths[:dim], size, lengths[dim] // size, *lengths[dim + 1 :])
    return jnp.moveaxis(parts, dim, 0)


def sum_packed(arrays, axis, dims):
    size = lax.axis_size(axis)
    parts = [in_blocks(a, dim, size) for a, dim in zip(arrays, dims)]
    lines = jnp.concatenate([b.reshape(size, -1) for b in parts], axis=1)
    extent = max(16, -(-lines.shape[1] // 1024) * 8)
    lines = jnp.pad(lines, ((0, 0), (0, extent * 128 - lines.shape[1]))).reshape(-1, 128)
    flat, at, outs = (lax.psum_scatter(lines, axis, tiled=True).reshape(-1), 0, [])
    for b in parts:
        part = b[0]
        outs.append(flat[at : at + part.size].reshape(part.shape))
        at += part.size
    return tuple(outs)


def split_heads(matrix):
    return matrix.reshape(matrix.shape[0], matrix.shape[1] // HEAD_DIM, HEAD_DIM)


def join_heads(tensor):
    return tensor.reshape(tensor.shape[0], tensor.shape[1] * tensor.shape[2])


def stats_update(running, query_heads, grad_heads, query_pos, key_block, value_block, key_pos):
    maximum, denominator, delta_sum = running
    scaling = HEAD_DIM ** (-0.5)
    scores = (
        jnp.einsum("qhd,khd->hqk", query_heads, key_block, preferred_element_type=jnp.float32)
        * scaling
    )
    allowed = (key_pos[None, :] <= query_pos[:, None])[None]
    masked = jnp.where(allowed, scores, -1e30)
    new_max = jnp.maximum(maximum, jnp.max(masked, axis=2))
    unscaled = jnp.where(allowed, jnp.exp(masked - new_max[:, :, None]), 0.0)
    grad_probs = jnp.einsum(
        "qhd,khd->hqk", grad_heads, value_block, preferred_element_type=jnp.float32
    )
    denominator = jnp.sum(unscaled, axis=2)
    delta_sum = jnp.sum(unscaled * grad_probs, axis=2)
    return (new_max, denominator, delta_sum)


def gradient_terms(
    query_heads, grad_heads, query_pos, log_total, row_delta, key_block, value_block, key_pos
):
    scaling = HEAD_DIM ** (-0.5)
    scores = (
        jnp.einsum("qhd,khd->hqk", query_heads, key_block, preferred_element_type=jnp.float32)
        * scaling
    )
    allowed = (key_pos[None, :] <= query_pos[:, None])[None]
    masked = jnp.where(allowed, scores, -1e30)
    probabilities = jnp.where(allowed, jnp.exp(masked - log_total[:, :, None]), 0.0)
    weights = probabilities.astype(jnp.bfloat16)
    grad_value = jnp.einsum("hqk,qhd->khd", weights, grad_heads, preferred_element_type=jnp.float32)
    grad_probs = jnp.einsum(
        "qhd,khd->hqk", grad_heads, value_block, preferred_element_type=jnp.float32
    )
    grad_scores = (probabilities * (grad_probs - row_delta[:, :, None]) * scaling).astype(
        jnp.bfloat16
    )
    grad_query = jnp.einsum(
        "hqk,khd->qhd", grad_scores, key_block, preferred_element_type=jnp.float32
    )
    grad_key = jnp.einsum(
        "hqk,qhd->khd", grad_scores, query_heads, preferred_element_type=jnp.float32
    )
    return (grad_query, grad_key, grad_value)


def local(query_rows, key_rows, value_rows, grad_output, positions):
    row_count = query_rows.shape[0]
    head_count = query_rows.shape[1] // HEAD_DIM
    members = lax.axis_size("seq")
    query_heads = split_heads(query_rows)
    grad_heads = split_heads(grad_output)
    start_running = (
        jnp.full((head_count, row_count), -1e30, jnp.float32),
        jnp.zeros((head_count, row_count), jnp.float32),
        jnp.zeros((head_count, row_count), jnp.float32),
    )
    start_copies = (
        jnp.zeros((row_count * members, key_rows.shape[1]), key_rows.dtype),
        jnp.zeros((row_count * members, value_rows.shape[1]), value_rows.dtype),
        jnp.zeros((row_count * members,), jnp.int32),
    )
    start_carry = (start_running, start_copies)
    portion = (
        *side_by_side((key_rows, value_rows), "seq", 0, 1),
        lax.all_gather(positions, "seq", axis=0, tiled=True),
    )
    offset = jnp.int32(0)
    stats = stats_update(
        start_carry[0],
        query_heads,
        grad_heads,
        positions,
        split_heads(portion[0]),
        split_heads(portion[1]),
        portion[2],
    )
    copies = tuple(
        (
            lax.dynamic_update_slice_in_dim(held_copy, piece, offset, 0)
            for held_copy, piece in zip(start_carry[1], portion)
        )
    )
    maximum, denominator, delta_sum = stats
    log_total = maximum + jnp.log(denominator)
    row_delta = delta_sum / denominator
    key_copy, value_copy, pos_copy = copies
    full_shape = (row_count * members, head_count, HEAD_DIM)

    def held_turn(block_index, carried):
        query_sum, key_full, value_full = carried
        begin = block_index * row_count
        key_block = split_heads(lax.dynamic_slice_in_dim(key_copy, begin, row_count, 0))
        value_block = split_heads(lax.dynamic_slice_in_dim(value_copy, begin, row_count, 0))
        pos_block = lax.dynamic_slice_in_dim(pos_copy, begin, row_count, 0)
        pieces = gradient_terms(
            query_heads,
            grad_heads,
            positions,
            log_total,
            row_delta,
            key_block,
            value_block,
            pos_block,
        )
        key_full = lax.dynamic_update_slice_in_dim(key_full, pieces[1], begin, 0)
        value_full = lax.dynamic_update_slice_in_dim(value_full, pieces[2], begin, 0)
        return (query_sum + pieces[0], key_full, value_full)

    start_held = (
        jnp.zeros((row_count, head_count, HEAD_DIM), jnp.float32),
        jnp.zeros(full_shape, jnp.float32),
        jnp.zeros(full_shape, jnp.float32),
    )
    grad_query, key_full, value_full = lax.fori_loop(0, members, held_turn, start_held)
    grad_keys, grad_values = sum_packed((key_full, value_full), "seq", (0, 0))
    regrouped = lax.all_to_all(
        join_heads(grad_query).astype(jnp.bfloat16), "head", split_axis=0, concat_axis=1, tiled=True
    )
    return (
        regrouped,
        join_heads(grad_keys).astype(jnp.bfloat16),
        join_heads(grad_values).astype(jnp.bfloat16),
    )


def solution(mesh):
    placed = (P("seq", "head"), P("seq", "head"), P("seq", "head"), P("seq", "head"), P("seq"))
    return jax.shard_map(
        local,
        mesh=mesh,
        in_specs=placed,
        out_specs=(P(("seq", "head"), None), P("seq", "head"), P("seq", "head")),
        check_vma=False,
    )
```

profile of v0, /device:TPU:1, one launch (start us, length us, event | category | flops | bytes accessed | tf_op | source)
XLA Modules:
  0.0 510.9 jit_solution(8410286546639562708)
XLA Ops:
  7.2 1.6 pad_maximum_fusion.1
  9.0 1.3 dynamic-slice
  11.8 108.2 %all-reduce = s32[6144]{0:T(1024)S(1)} all-reduce(s32[6144]{0:T(1024)S(1)} %dynamic-update-slice), channel_id=1, replica_groups=mesh['seq'=32,'head'=8] {'seq'}, use_global_device_ids=true, to_apply=%add | all-reduce | flops 6144 | bytes 49152
  121.0 1.4 broadcast_compare_fusion.1
  122.4 5.8 %fusion.19 = (bf16[6144,256]{1,0:T(8,128)(2,1)}, bf16[6144,256]{1,0:T(8,128)(2,1)}) fusion(bf16[6144,512]{1,0:T(8,128)(2,1)} %all-gather.2.cloned.1.call-done), kind=kLoop, calls=%fused_computation.39 | loop fusion | bytes 12582912 | tf_op jit(solution)/shard_map/split | solution.py:15
  128.2 4.7 copy.73
  132.9 7.9 %fusion.22 = (f32[2,192]{1,0:T(2,128)S(1)}, f32[2,192,6144]{2,1,0:T(8,128)}) fusion(bf16[6144,2,128]{0,2,1:T(8,128)(2,1)} %bitcast.118, pred[192,6144]{1,0:T(8,128)(4,1)S(1)} %broadcast_compare_fusion.1, bf16[192,256]{1,0:T(8,128)(2,1)S(1)} %copy-done), kind=kOutput, calls=%fused_computation.42 | convolution fusion | flops 611057280 | bytes 13862400 | tf_op jit(solution)/shard_map/qhd,khd->hqk/dot_general | solution.py:50
  140.8 4.7 copy.74
  145.5 6.2 %fusion.18 = f32[2,192]{1,0:T(2,128)S(1)} fusion(f32[2,192,6144]{2,1,0:T(8,128)} %get-tuple-element.315, f32[2,192]{1,0:T(2,128)S(1)} %broadcast_maximum_fusion, pred[192,6144]{1,0:T(8,128)(4,1)S(1)} %broadcast_compare_fusion.1), kind=kLoop, calls=%fused_computation.32 | loop fusion | flops 7077504 | bytes 10619904 | tf_op jit(solution)/shard_map/reduce_sum | solution.py:60
  151.9 5.4 %fusion.17 = f32[2,192]{1,0:T(2,128)S(1)} fusion(bf16[6144,2,128]{0,2,1:T(8,128)(2,1)} %bitcast.119, f32[2,192,6144]{2,1,0:T(8,128)S(1)} %copy-done.2, f32[2,192]{1,0:T(2,128)S(1)} %broadcast_maximum_fusion, pred[192,6144]{1,0:T(8,128)(4,1)S(1)} %broadcast_compare_fusion.1, bf16[192,256]{1,0:T(8,128)(2,1)S(1)} %copy-done.3), kind=kOutput, calls=%fused_computation.29 | convolution fusion | flops 613416576 | bytes 13863936 | tf_op jit(solution)/shard_map/qhd,khd->hqk/dot_general | solution.py:57
  157.3 4.1 broadcast.63.clone
  161.5 4.2 broadcast.63.clone2
  165.6 164.9 %while.18 = (s32[]{:T(128)}, f32[192,2,128]{2,0,1:T(8,128)S(1)}, f32[6144,2,128]{2,1,0:T(2,128)}, f32[6144,2,128]{2,1,0:T(2,128)}, bf16[6144,256]{1,0:T(8,128)(2...) while((s32[]{:T(128)}, f32[192,2,128]{2,0,1:T(8,128)S(1)}, ...), condition=%wide.region_4.5_spmd.clone, body=%wide.region_3.4_spmd.clone.sunk | while | flops 95170560 | bytes 3668193 | solution.py:161
  165.8 1.2 fusion.58
  171.0 1.2 fusion.58
  181.3 1.2 fusion.58
  207.0 1.2 fusion.58
  227.6 1.2 fusion.58
  232.8 1.2 fusion.58
  243.1 1.2 fusion.58
  248.3 1.2 fusion.58
  253.5 1.2 fusion.58
  263.8 1.2 fusion.58
  274.1 1.2 fusion.58
  279.2 1.2 fusion.58
  310.1 1.2 fusion.58
  330.5 8.7 %reshape_reshape.8 = f32[32,49152]{1,0:T(8,128)} reshape(f32[6144,2,128]{2,1,0:T(2,128)} %get-tuple-element.205) | data formatting | bytes 12582912 | tf_op jit(solution)/shard_map/reshape;reshape | solution.py:27
  339.2 8.5 %reshape_reshape.9 = f32[32,49152]{1,0:T(8,128)} reshape(f32[6144,2,128]{2,1,0:T(2,128)} %get-tuple-element.206) | data formatting | bytes 12582912 | tf_op jit(solution)/shard_map/reshape;reshape | solution.py:27
  347.6 10.0 %pad_maximum_fusion = f32[32,98304]{1,0:T(8,128)} fusion(f32[32,49152]{1,0:T(8,128)} %reshape_reshape.9, f32[32,49152]{1,0:T(8,128)} %reshape_reshape.8), kind=kLoop, calls=%fused_computation.27 | loop fusion | flops 3145728 | bytes 25165824 | tf_op jit(solution)/shard_map/concatenate | solution.py:27
  357.6 9.7 %reshape.111 = f32[24576,128]{1,0:T(8,128)} reshape(f32[32,98304]{1,0:T(8,128)} %pad_maximum_fusion) | data formatting | bytes 25165824 | tf_op jit(solution)/shard_map/reshape | solution.py:29
  367.5 13.7 %all_to_all.16 = bf16[8,24,256]{2,1,0:T(8,128)(2,1)S(1)} all-to-all(bf16[8,24,256]{2,1,0:T(8,128)(2,1)S(1)} %convert_element_type.30), channel_id=1, replica_groups=mesh['seq'=32,'head'=8] {'head'}, dimensions={0} | all-to-all | bytes 196608 | tf_op jit(solution)/shard_map/all_to_all | solution.py:163
  381.9 119.7 %reduce-scatter.2.cloned.1.call-done = f32[768,128]{1,0:T(8,128)} async-done(((f32[24576,128]{1,0:T(8,128)}), f32[768,128]{1,0:T(8,128)}) %reduce-scatter.2.cloned.1.call-update) | async-done | bytes 393232 | tf_op jit(solution)/shard_map/reduce_scatter | solution.py:30
  (272 shorter events, 153.0 us)
Async XLA Ops:
  7.2 112.9 %copy-start = (bf16[192,256]{1,0:T(8,128)(2,1)S(1)}, bf16[192,256]{1,0:T(8,128)(2,1)}, u32[]{:S(2)}) copy-start(bf16[192,256]{1,0:T(8,128)(2,1)} %param.7) | copy-start | bytes 294916
  7.2 115.2 %all-gather.2.cloned.1.call-start = ((), (), s32[]{:S(2)}) async-start(), calls=%async_computation.2 | async-start | bytes 6488064 | tf_op jit(solution)/shard_map/all_gather | solution.py:15
  8.9 492.7 %reduce-scatter.2.cloned.1.call-start = ((), (), s32[]{:S(2)}) async-start(), calls=%async_computation.3 | async-start | bytes 12976128 | tf_op jit(solution)/shard_map/reduce_scatter | solution.py:30
  145.5 6.4 %copy-start.2 = (f32[2,192,6144]{2,1,0:T(8,128)S(1)}, f32[2,192,6144]{2,1,0:T(8,128)}, u32[]{:S(2)}) copy-start(f32[2,192,6144]{2,1,0:T(8,128)} %get-tuple-element.315) | copy-start | bytes 28311556
  145.5 6.4 %copy-start.3 = (bf16[192,256]{1,0:T(8,128)(2,1)S(1)}, bf16[192,256]{1,0:T(8,128)(2,1)}, u32[]{:S(2)}) copy-start(bf16[192,256]{1,0:T(8,128)(2,1)} %param.10) | copy-start | bytes 294916
  157.3 8.3 %copy-start.4 = (s32[192]{0:T(256)S(1)}, s32[192]{0:T(256)}, u32[]{:S(2)}) copy-start(s32[192]{0:T(256)} %param.11) | copy-start | bytes 2308
  367.3 136.7 %copy-start.1 = (bf16[192,256]{1,0:T(8,128)(2,1)S(1)}, bf16[192,256]{1,0:T(8,128)(2,1)}, u32[]{:S(2)}) copy-start(bf16[192,256]{1,0:T(8,128)(2,1)} %param.7) | copy-start | bytes 294916
Sparse Core Ops, SparseCore 0:
  9.8 73.4 all-gather.1
  367.4 134.1 reduce-scatter.1
where the time goes:
time: 517 us; the launch traced here: 511 us
  matrix products  136 us (26%)
  blocking collectives  122 us (24%)
  waiting for transfers between devices  120 us (23%)
  local copies, waits for them, and re-layouts  92.4 us (18%)
  other arithmetic  23.4 us (5%)
  between operations  14.8 us (3%)
    reduce_scatter x1, waiting for transfers between devices, sum_packed(): lax.psum_scatter(lines, axis, tiled=True).reshape(-1)  120 us
    unnamed x1, blocking collectives  108 us
    dot_general x32, matrix products, gradient_terms(): jnp.einsum('qhd,khd->hqk', query_heads, key_block, preferred_element_type...  37.3 us
    dot_general x32, matrix products, gradient_terms(): jnp.einsum('hqk,khd->qhd', grad_scores, key_block, preferred_element_type...  37.2 us
    dot_general x32, matrix products, gradient_terms(): jnp.einsum('qhd,khd->hqk', grad_heads, value_block, preferred_element_typ...  36.1 us
    dynamic_update_slice x32, local copies, waits for them, and re-layouts, held_turn(): lax.dynamic_update_slice_in_dim(value_full, pieces[2], begin, 0)  34.2 us
    another operation x2, local copies, waits for them, and re-layouts, sum_packed(): lines = jnp.concatenate([b.reshape(size, -1) for b in parts], axis=1)  17.1 us
    all_to_all x1, blocking collectives, local(): lax.all_to_all(join_heads(grad_query).astype(jnp.bfloat16), 'head', split...  13.7 us
  transfers between devices with their start and end apart: 2, of which 1 were waited for; matrix products, arithmetic and copies ran while one was open for 1% of the time, Pallas kernels for 0%

commit v1 on v0

v1 whole, which is shorter than its diff:
```python
import math

import jax
import jax.numpy as jnp
from jax import lax
from jax.experimental import pallas as pl
from jax.experimental.pallas import tpu as pltpu
from jax.sharding import PartitionSpec as P

MESH = pl.DeviceIdType.MESH
HEAD_DIM = 128
SCALE = HEAD_DIM**-0.5
SCALE2 = SCALE * math.log2(math.e)
FAR = -1e30
Z = 8
HOPS = 7
F32, BF16 = jnp.float32, jnp.bfloat16
NT = (((1,), (1,)), ((), ()))
TN = (((0,), (0,)), ((), ()))


def kernel(
    q_ref, k_ref, v_ref, g_ref, pos_ref, dq_ref, dk_ref, dv_ref,
    kvg, xkv, xq, qd, qf, gf, st, dpt, qpos, mx, tot, dsum, dqt,
    sibs, sibr, part, snd, rcv, xs, xr, dqs, dqr,
    in_recv, z_send, sib_send, x_send, q_recv, g_send, g_recv,
    r_send, r_recv, xr_send, xr_recv, d_send, d_recv,
):
    rows = q_ref.shape[0]
    me, hd = lax.axis_index("seq"), lax.axis_index("head")
    heads = lax.axis_size("head")
    x, z, c = lax.div(me, 16), lax.div(lax.rem(me, 16), 2), lax.rem(me, 2)

    def dev(xx, zz, cc):
        return xx * 16 + zz * 2 + cc

    up, down = dev(x, lax.rem(z + 1, Z), c), dev(x, lax.rem(z + Z - 1, Z), c)
    sibling, across = dev(x, z, 1 - c), dev(1 - x, z, c)

    def push(src, dst, send, recv, seq, head=hd):
        return pltpu.make_async_remote_copy(
            src_ref=src, dst_ref=dst, send_sem=send, recv_sem=recv,
            device_id={"seq": seq, "head": head}, device_id_type=MESH,
        )

    mine, other = pl.multiple_of(x * 128, 128), pl.multiple_of((1 - x) * 128, 128)
    kvg[me, 0:rows] = k_ref[:, pl.ds(mine, 128)]
    kvg[me, rows : 2 * rows] = v_ref[:, pl.ds(mine, 128)]
    kvg[me, 2 * rows : 2 * rows + 16] = pos_ref[...]
    xkv[0:rows] = k_ref[:, pl.ds(other, 128)]
    xkv[rows : 2 * rows] = v_ref[:, pl.ds(other, 128)]
    xkv[2 * rows : 2 * rows + 16] = pos_ref[...]
    qd[x, 0] = q_ref[:, pl.ds(mine, 128)]
    qd[x, 1] = g_ref[:, pl.ds(mine, 128)]
    xq[0] = q_ref[:, pl.ds(other, 128)]
    xq[1] = g_ref[:, pl.ds(other, 128)]

    flat = x * heads + hd

    def peer(r):
        there = lax.rem(flat + r, 2 * heads)
        return lax.div(there, heads), lax.rem(there, heads)

    barrier = pltpu.get_barrier_semaphore()
    for seq in (up, down, sibling):
        pl.semaphore_signal(barrier, inc=1, device_id={"seq": seq, "head": hd}, device_id_type=MESH)
    for r in range(1, 2 * heads):
        xx, gg = peer(r)
        pl.semaphore_signal(barrier, inc=1, device_id={"seq": dev(xx, z, c), "head": gg}, device_id_type=MESH)
    pl.semaphore_wait(barrier, 3 + 2 * heads - 1)

    def z_copy(way, s):
        return push(kvg.at[s], kvg.at[s], z_send.at[way, s], in_recv.at[s], up if way == 0 else down)

    def sib_copy(s):
        return push(kvg.at[s], kvg.at[s], sib_send.at[s], in_recv.at[s], sibling)

    partner = dev(1 - x, z, c)
    x_copy = push(xkv, kvg.at[me], x_send.at[0], in_recv.at[me], across)
    q_copy = push(xq, qd.at[x], x_send.at[1], q_recv, across)
    z_copy(0, me).start()
    z_copy(1, me).start()
    x_copy.start()
    sib_copy(me).start()
    q_copy.start()

    def arrive(s):
        sib_copy(s).wait_recv()

    mx[...] = jnp.full(mx.shape, FAR, F32)
    tot[...] = jnp.zeros(tot.shape, F32)
    dsum[...] = jnp.zeros(dsum.shape, F32)
    dqt[...] = jnp.zeros(dqt.shape, F32)

    def key_positions(s):
        block = kvg[s, 2 * rows : 2 * rows + 16].astype(F32)
        first = block[0:1] * 64.0 + block[2:3]
        rest = block[1:2] * 64.0 + block[3:4]
        columns = jnp.concatenate(
            [jnp.broadcast_to(first, (128, 128)).T, jnp.broadcast_to(rest, (128, 128)).T[0 : rows - 128]], axis=0
        )
        return columns

    def scores(s):
        raw = lax.dot_general(kvg[s, 0:rows], qf[...], NT, preferred_element_type=F32)
        grad_probs = lax.dot_general(kvg[s, rows : 2 * rows], gf[...], NT, preferred_element_type=F32)
        columns = key_positions(s)
        columns = jnp.concatenate([columns] * (2 * rows // 128), axis=1)
        raw = jnp.where(columns <= qpos[0:1], raw, FAR)
        st[s] = raw
        dpt[s] = grad_probs
        before = mx[0:1]
        top = jnp.maximum(before, jnp.max(raw, axis=0, keepdims=True))
        fade = jnp.exp2((before - top) * SCALE2)
        p = jnp.exp2((raw - top) * SCALE2)
        mx[0:1] = top
        tot[0:1] = tot[0:1] * fade + jnp.sum(p, axis=0, keepdims=True)
        dsum[0:1] = dsum[0:1] * fade + jnp.sum(p * grad_probs, axis=0, keepdims=True)

    arrive(partner)
    z_copy(0, partner).start()
    z_copy(1, partner).start()
    sib_copy(partner).start()
    q_copy.wait_recv()
    for xx in range(2):
        qf[xx * rows : (xx + 1) * rows] = qd[xx, 0]
        gf[xx * rows : (xx + 1) * rows] = qd[xx, 1]
    both = jnp.concatenate([key_positions(dev(0, z, c)), key_positions(dev(1, z, c))], axis=0)
    qpos[...] = both.T[0:8]

    def sub_of(way, e):
        far = lax.div(e, 2) + 1
        kind = lax.rem(e, 2) if way == 0 else jnp.where(e < 6, lax.rem(e, 2), 1)
        xx = x + kind - 2 * x * kind
        zz = lax.rem(z + Z - far, Z) if way == 0 else lax.rem(z + far, Z)
        return xx, zz

    def gather_step(e, carry):
        for way in range(2):
            xx, zz = sub_of(way, e)
            s = dev(xx, zz, c)
            arrive(s)
            onward = e <= 4 if way == 0 else jnp.logical_or(e <= 3, e == 5)

            @pl.when(onward)
            def _():
                z_copy(way, s).start()

            sib_copy(s).start()

        @pl.when(e == 0)
        def _():
            scores(me)
            scores(partner)

        for way in range(2):
            xx, zz = sub_of(way, e)
            scores(dev(xx, zz, c))
        for way in range(2):
            xx, zz = sub_of(way, jnp.maximum(e - 1, 0))
            first = e == 0
            xx = jnp.where(first, way, xx)
            zz = jnp.where(first, z, zz)
            s = dev(xx, zz, 1 - c)
            arrive(s)
            scores(s)
        return carry

    lax.fori_loop(0, HOPS, gather_step, 0)
    for way in range(2):
        xx, zz = sub_of(way, jnp.int32(HOPS - 1))
        s = dev(xx, zz, 1 - c)
        arrive(s)
        scores(s)

    total = tot[0:1]
    mx[0:1] = mx[0:1] * SCALE2 + jnp.log2(total)
    dsum[0:1] = dsum[0:1] / total

    def grads(s):
        p = jnp.exp2(st[s] * SCALE2 - mx[0:1])
        grad_scores = (p * (dpt[s] - dsum[0:1])).astype(BF16)
        dv = jnp.dot(p.astype(BF16), gf[...], preferred_element_type=F32)
        dk = jnp.dot(grad_scores, qf[...], preferred_element_type=F32) * SCALE
        dqt[...] += lax.dot_general(kvg[s, 0:rows], grad_scores, TN, preferred_element_type=F32)
        return dk, dv

    def g_copy(n):
        return push(sibs.at[n], sibr.at[n], g_send.at[n], g_recv.at[n], sibling)

    def r_copy(way, i):
        return push(snd.at[way, i], rcv.at[way, i], r_send.at[way, i], r_recv.at[way, i], up if way == 0 else down)

    def goal(way, i):
        far = 4 - lax.div(i + 1, 2)
        kind = lax.rem(i, 2) if way == 0 else 1 - lax.rem(i, 2)
        xx = x + kind - 2 * x * kind
        zz = lax.rem(z + far, Z) if way == 0 else lax.rem(z + Z - far, Z)
        return xx, zz

    def reduce_step(i, carry):
        for way in range(2):
            xx, zz = goal(way, i)
            dk, dv = grads(dev(xx, zz, 1 - c))
            n = 2 * i + way
            sibs[n, :, 0:128] = dk.astype(BF16)
            sibs[n, :, 128:256] = dv.astype(BF16)
            g_copy(n).start()
        for way in range(2):
            xx, zz = goal(way, i)
            dk, dv = grads(dev(xx, zz, c))
            part[way, :, 0:128] = dk
            part[way, :, 128:256] = dv
        for way in range(2):
            n = 2 * i + way
            g_copy(n).wait_recv()
            part[way] = part[way] + sibr[n].astype(F32)

            @pl.when(jnp.logical_and(i >= 2, i < HOPS))
            def _():
                r_copy(way, i - 2).wait_recv()
                part[way] = part[way] + rcv[way, i - 2].astype(F32)

            @pl.when(i < HOPS)
            def _():
                snd[way, i] = part[way].astype(BF16)
                r_copy(way, i).start()

        return carry

    lax.fori_loop(0, HOPS + 1, reduce_step, 0)

    grad_query = dqt[...].T * SCALE
    few = rows // heads
    for n in range(2 * heads):
        dqs[n] = grad_query[n * few : (n + 1) * few].astype(BF16)
    column = hd * 2 + x

    def d_copy(r):
        xx, gg = peer(r)
        n = xx * heads + gg
        return push(dqs.at[n], dqr.at[column], d_send.at[n], d_recv.at[column], dev(xx, z, c), gg)

    def d_wait(r):
        xx, gg = peer(r)
        source = gg * 2 + xx
        return push(dqs.at[0], dqr.at[source], d_send.at[0], d_recv.at[source], dev(xx, z, c), gg)

    for r in range(1, 2 * heads):
        d_copy(r).start()
    dqr[column] = dqs[flat]

    r_copy(0, 5).wait_recv()
    r_copy(1, 6).wait_recv()
    xs[...] = (part[0] + rcv[0, 5].astype(F32) + rcv[1, 6].astype(F32)).astype(BF16)
    xr_copy = push(xs, xr, xr_send, xr_recv, across)
    xr_copy.start()
    r_copy(0, 6).wait_recv()
    r_copy(1, 5).wait_recv()
    own = (part[1] + rcv[0, 6].astype(F32) + rcv[1, 5].astype(F32)).astype(BF16)
    dk_ref[:, pl.ds(mine, 128)] = own[:, 0:128]
    dv_ref[:, pl.ds(mine, 128)] = own[:, 128:256]

    for r in range(1, 2 * heads):
        d_wait(r).wait_recv()
    for n in range(2 * heads):
        dq_ref[:, n * 128 : (n + 1) * 128] = dqr[n]
    xr_copy.wait_recv()
    dk_ref[:, pl.ds(other, 128)] = xr[:, 0:128]
    dv_ref[:, pl.ds(other, 128)] = xr[:, 128:256]

    x_copy.wait_send()
    q_copy.wait_send()
    xr_copy.wait_send()
    for way in range(2):
        z_copy(way, me).wait_send()
        z_copy(way, partner).wait_send()
    sib_copy(me).wait_send()
    sib_copy(partner).wait_send()

    def drain_gather(e, carry):
        for way in range(2):
            xx, zz = sub_of(way, e)
            s = dev(xx, zz, c)
            onward = e <= 4 if way == 0 else jnp.logical_or(e <= 3, e == 5)

            @pl.when(onward)
            def _():
                z_copy(way, s).wait_send()

            sib_copy(s).wait_send()
            r_copy(way, e).wait_send()
        return carry

    lax.fori_loop(0, HOPS, drain_gather, 0)

    def drain_sums(n, carry):
        g_copy(n).wait_send()
        return carry

    lax.fori_loop(0, 2 * HOPS + 2, drain_sums, 0)
    for r in range(1, 2 * heads):
        d_copy(r).wait_send()


def local(query_rows, key_rows, value_rows, grad_output, positions):
    rows, width = query_rows.shape
    heads = lax.axis_size("head")
    members = lax.axis_size("seq")
    padded = jnp.pad(positions, (0, 256 - rows))
    coded = jnp.concatenate([padded // 64, padded % 64]).astype(BF16).reshape(4, 128)
    coded = jnp.pad(coded, ((0, 12), (0, 0)))
    vmem = pl.BlockSpec(memory_space=pltpu.VMEM)
    dma, tall = pltpu.SemaphoreType.DMA, 2 * rows + 16
    few = rows // heads
    return pl.pallas_call(
        kernel,
        out_shape=(
            jax.ShapeDtypeStruct((few, heads * width), BF16),
            jax.ShapeDtypeStruct((rows, width), BF16),
            jax.ShapeDtypeStruct((rows, width), BF16),
        ),
        in_specs=[vmem] * 5,
        out_specs=(vmem,) * 3,
        scratch_shapes=[
            pltpu.VMEM((members, tall, 128), BF16),
            pltpu.VMEM((tall, 128), BF16),
            pltpu.VMEM((2, rows, 128), BF16),
            pltpu.VMEM((2, 2, rows, 128), BF16),
            pltpu.VMEM((2 * rows, 128), BF16),
            pltpu.VMEM((2 * rows, 128), BF16),
            pltpu.VMEM((members, rows, 2 * rows), F32),
            pltpu.VMEM((members, rows, 2 * rows), F32),
            pltpu.VMEM((8, 2 * rows), F32),
            pltpu.VMEM((8, 2 * rows), F32),
            pltpu.VMEM((8, 2 * rows), F32),
            pltpu.VMEM((8, 2 * rows), F32),
            pltpu.VMEM((128, 2 * rows), F32),
            pltpu.VMEM((16, rows, 256), BF16),
            pltpu.VMEM((16, rows, 256), BF16),
            pltpu.VMEM((2, rows, 256), F32),
            pltpu.VMEM((2, HOPS, rows, 256), BF16),
            pltpu.VMEM((2, HOPS, rows, 256), BF16),
            pltpu.VMEM((rows, 256), BF16),
            pltpu.VMEM((rows, 256), BF16),
            pltpu.VMEM((2 * heads, few, 128), BF16),
            pltpu.VMEM((2 * heads, few, 128), BF16),
            dma((members,)),
            dma((2, members)),
            dma((members,)),
            dma((2,)),
            dma,
            dma((16,)),
            dma((16,)),
            dma((2, HOPS)),
            dma((2, HOPS)),
            dma,
            dma,
            dma((2 * heads,)),
            dma((2 * heads,)),
        ],
        compiler_params=pltpu.CompilerParams(
            collective_id=0, has_side_effects=True, vmem_limit_bytes=60 * 1024 * 1024
        ),
    )(query_rows, key_rows, value_rows, grad_output, coded)


def solution(mesh):
    placed = (P("seq", "head"), P("seq", "head"), P("seq", "head"), P("seq", "head"), P("seq"))
    return jax.shard_map(
        local,
        mesh=mesh,
        in_specs=placed,
        out_specs=(P(("seq", "head"), None), P("seq", "head"), P("seq", "head")),
        check_vma=False,
    )
```

time: 517 us -> 65.5 us (0.13); the launches traced: 511 us -> 65.3 us
  matrix products: 136 us -> 0 us
  blocking collectives: 122 us -> 0 us
  waiting for transfers between devices: 120 us -> 0 us
  local copies, waits for them, and re-layouts: 92.4 us -> 3.15 us
  Pallas kernels: 0 us -> 60.2 us
  other arithmetic: 23.4 us -> 1.3 us
  between operations: 14.8 us -> 0.65 us
    dot_general x162 -> x0, matrix products: 136 us -> none  [the longest x32 37.3 us: gradient_terms(): jnp.einsum('qhd,khd->hqk', query_heads, key_block, preferred_element_type...]
    reduce_scatter x1 -> x0, waiting for transfers between devices: 120 us -> none  [sum_packed(): lax.psum_scatter(lines, axis, tiled=True).reshape(-1)]
    unnamed x1 -> x0, blocking collectives: 108 us -> none
    pallas_call x0 -> x1, Pallas kernels: none -> 60.2 us  [local(): pl.pallas_call(kernel, out_shape=(jax.ShapeDtypeStruct((few, heads * widt...]
    dynamic_update_slice x32 -> x0, local copies, waits for them, and re-layouts: 34.2 us -> none  [held_turn(): lax.dynamic_update_slice_in_dim(value_full, pieces[2], begin, 0)]
    another operation x4 -> x0, local copies, waits for them, and re-layouts: 25.4 us -> none  [the longest x2 17.1 us: sum_packed(): lines = jnp.concatenate([b.reshape(size, -1) for b in parts], axis=1)]
    all_to_all x1 -> x0, blocking collectives: 13.7 us -> none  [local(): lax.all_to_all(join_heads(grad_query).astype(jnp.bfloat16), 'head', split...]
    concatenate x2, other arithmetic: 11.6 us -> 1.3 us  [local(): jnp.concatenate([padded // 64, padded % 64]).astype(BF16).reshape(4, 128)]
  transfers between devices with their start and end apart: 2 -> 0, of which waited for: 1 -> 0; matrix products, arithmetic and copies ran while one was open for 1% -> 0% of each run, Pallas kernels for 0% -> 0%
where the time goes in v1:
time: 65.5 us; the launch traced here: 65.3 us
  Pallas kernels  60.2 us (92%)
  local copies, waits for them, and re-layouts  3.15 us (5%)
  other arithmetic  1.3 us (2%)
    pallas_call x1, Pallas kernels, local(): pl.pallas_call(kernel, out_shape=(jax.ShapeDtypeStruct((few, heads * widt...  60.2 us
    unnamed x7, local copies, waits for them, and re-layouts  3.15 us

profile of v1, /device:TPU:1, one launch (start us, length us, event | category | flops | bytes accessed | tf_op | source)
XLA Modules:
  0.0 65.3 jit_solution(7004521177672964492)
XLA Ops:
  0.6 0.7 %fusion.6 = (bf16[2,128]{1,0:T(2,128)(2,1)S(1)}, bf16[2,128]{1,0:T(2,128)(2,1)S(1)}) fusion(s32[192]{0:T(256)} %param.9), kind=kLoop, calls=%fused_computation.14 | loop fusion | flops 5376 | bytes 1792 | tf_op jit(solution)/shard_map/concatenate | solution.py:311
  1.3 0.6 fusion.2.pos_ref
  1.9 60.2 %shard_map.76 = (bf16[24,2048]{1,0:T(8,128)(2,1)}, bf16[192,256]{1,0:T(8,128)(2,1)}, bf16[192,256]{1,0:T(8,128)(2,1)}) custom-call(bf16[192,256]{1,0:T(8,128)(2,1)} %q_ref.1, bf16[192,256]{1,0:T(8,128)(2,1)} %k_ref.1, bf16[192,256]{1,0:T(8,128)(2,1)} %v_ref.1, bf16[192,256]{1,0:T(8,128)(2,1)} %g_ref.1, bf16[16,128]{1,0:T(8,128)(2,1)} %fusion.2.pos_ref), custom_call_target="tpu_custom_call" | custom-call | tf_op jit(solution)/shard_map/pallas_call | solution.py:316
  62.2 0.0 copy-start.1
  62.2 1.6 %copy.11 = bf16[24,2048]{1,0:T(8,128)(2,1)} copy(bf16[24,2048]{1,0:T(8,128)(2,1)} %get-tuple-element.8) | data formatting | bytes 196608
  63.8 0.0 copy-done.1
  63.8 0.0 copy-start
  63.8 0.6 copy.12
  64.4 0.3 copy-done
  64.7 0.6 copy.13
Async XLA Ops:
  62.2 1.6 %copy-start.1 = (bf16[192,256]{1,0:T(8,128)(2,1)S(1)}, bf16[192,256]{1,0:T(8,128)(2,1)}, u32[]{:S(2)}) copy-start(bf16[192,256]{1,0:T(8,128)(2,1)} %get-tuple-element.9) | copy-start | bytes 294916
  63.8 0.9 %copy-start = (bf16[192,256]{1,0:T(8,128)(2,1)S(1)}, bf16[192,256]{1,0:T(8,128)(2,1)}, u32[]{:S(2)}) copy-start(bf16[192,256]{1,0:T(8,128)(2,1)} %get-tuple-element.10) | copy-start | bytes 294916

commit v2 on v1

v2 whole, which is shorter than its diff:
```python
import math

import jax
import jax.numpy as jnp
from jax import lax
from jax.experimental import pallas as pl
from jax.experimental.pallas import tpu as pltpu
from jax.sharding import PartitionSpec as P

MESH = pl.DeviceIdType.MESH
HEAD_DIM = 128
SCALE = HEAD_DIM**-0.5
SCALE2 = SCALE * math.log2(math.e)
FAR = -1e30
Z = 8
F32, BF16 = jnp.float32, jnp.bfloat16
NT = (((1,), (1,)), ((), ()))
TN = (((0,), (0,)), ((), ()))


def kernel(
    q_ref, k_ref, v_ref, g_ref, pos_ref, dq_ref, dk_ref, dv_ref,
    kvg, xkv, xq, qf, gf, posr, posb, st, dpt, qpos, mx, tot, dsum, dqt,
    sibs, sibr, part, snd, rcv, xs, xr, dqs, dqr,
    l_sem, in_recv, z_send, sib_send, x_send, q_recv, g_send, g_recv,
    r_send, r_recv, xr_send, xr_recv, d_send, d_recv,
):
    rows = q_ref.shape[0]
    me, hd = lax.axis_index("seq"), lax.axis_index("head")
    heads = lax.axis_size("head")
    x, z, c = lax.div(me, 16), lax.div(lax.rem(me, 16), 2), lax.rem(me, 2)

    def dev(xx, zz, cc):
        return xx * 16 + zz * 2 + cc

    up, down = dev(x, lax.rem(z + 1, Z), c), dev(x, lax.rem(z + Z - 1, Z), c)
    sibling, across = dev(x, z, 1 - c), dev(1 - x, z, c)
    partner = across

    def push(src, dst, send, recv, seq, head=hd):
        return pltpu.make_async_remote_copy(
            src_ref=src, dst_ref=dst, send_sem=send, recv_sem=recv,
            device_id={"seq": seq, "head": head}, device_id_type=MESH,
        )

    vals, keys, tail = pl.ds(0, rows), pl.ds(rows, rows), pl.ds(2 * rows, 16)
    cut = (pl.ds(0, rows), pl.ds(rows, rows + 16))

    mine, other = pl.multiple_of(x * 128, 128), pl.multiple_of((1 - x) * 128, 128)
    held = pl.ds(pl.multiple_of(x * rows, rows), rows)
    loads = [
        pltpu.make_async_copy(src, dst, l_sem.at[n])
        for n, (src, dst) in enumerate((
            (pos_ref, posr),
            (v_ref.at[:, pl.ds(mine, 128)], kvg.at[me, vals]),
            (v_ref.at[:, pl.ds(other, 128)], xkv.at[vals]),
            (k_ref.at[:, pl.ds(mine, 128)], kvg.at[me, keys]),
            (k_ref.at[:, pl.ds(other, 128)], xkv.at[keys]),
            (q_ref.at[:, pl.ds(other, 128)], xq.at[0]),
            (g_ref.at[:, pl.ds(other, 128)], xq.at[1]),
            (q_ref.at[:, pl.ds(mine, 128)], qf.at[held]),
            (g_ref.at[:, pl.ds(mine, 128)], gf.at[held]),
        ))
    ]
    for load in loads:
        load.start()

    flat = x * heads + hd

    def peer(r):
        there = lax.rem(flat + r, 2 * heads)
        return lax.div(there, heads), lax.rem(there, heads)

    barrier = pltpu.get_barrier_semaphore()
    for seq in (up, down, sibling):
        pl.semaphore_signal(barrier, inc=1, device_id={"seq": seq, "head": hd}, device_id_type=MESH)
    for r in range(1, 2 * heads):
        xx, gg = peer(r)
        pl.semaphore_signal(barrier, inc=1, device_id={"seq": dev(xx, z, c), "head": gg}, device_id_type=MESH)

    mx[...] = jnp.full(mx.shape, FAR, F32)
    tot[...] = jnp.zeros(tot.shape, F32)
    dsum[...] = jnp.zeros(dsum.shape, F32)
    dqt[...] = jnp.zeros(dqt.shape, F32)

    loads[0].wait()
    place = posr[...].astype(F32)
    high = jnp.floor(place * (1.0 / 64.0))
    low = place - 64.0 * high
    posb[...] = jnp.zeros(posb.shape, F32)
    for n, digit in enumerate((high, low)):
        posb[2 * n : 2 * n + 1, :] = digit[:, 0:128]
        posb[2 * n + 1 : 2 * n + 2, 0 : rows - 128] = digit[:, 128:rows]
    kvg[me, tail] = posb[...].astype(BF16)
    xkv[tail] = posb[...].astype(BF16)

    pl.semaphore_wait(barrier, 3 + 2 * heads - 1)

    def z_copy(way, s, n, p):
        return push(kvg.at[s, cut[p]], kvg.at[s, cut[p]], z_send.at[way, n, p], in_recv.at[s, p], (up, down)[way])

    def sib_copy(s, n, p):
        return push(kvg.at[s, cut[p]], kvg.at[s, cut[p]], sib_send.at[n, p], in_recv.at[s, p], sibling)

    def x_copy(p):
        return push(xkv.at[cut[p]], kvg.at[me, cut[p]], x_send.at[p], in_recv.at[me, p], across)

    def q_copy(n):
        return push(xq.at[n], (qf, gf)[n].at[held], x_send.at[2 + n], q_recv.at[n], across)

    for p in range(2):
        loads[1 + 2 * p].wait()
        z_copy(0, me, 0, p).start()
        z_copy(1, me, 0, p).start()
        loads[2 + 2 * p].wait()
        x_copy(p).start()
        sib_copy(me, 0, p).start()
    for n in range(2):
        loads[5 + n].wait()
        q_copy(n).start()

    def arrive(s, p):
        sib_copy(s, 0, p).wait_recv()

    def key_positions(s):
        block = kvg[s, 2 * rows : 2 * rows + 16].astype(F32)
        first = block[0:1] * 64.0 + block[2:3]
        rest = block[1:2] * 64.0 + block[3:4]
        return jnp.concatenate(
            [jnp.broadcast_to(first, (128, 128)).T, jnp.broadcast_to(rest, (128, 128)).T[0 : rows - 128]], axis=0
        )

    def scores(s):
        raw = lax.dot_general(kvg[s, keys], qf[...], NT, preferred_element_type=F32)
        grad_probs = lax.dot_general(kvg[s, vals], gf[...], NT, preferred_element_type=F32)
        columns = key_positions(s)
        columns = jnp.concatenate([columns] * (2 * rows // 128), axis=1)
        raw = jnp.where(columns <= qpos[0:1], raw, FAR)
        st[s] = raw
        dpt[s] = grad_probs
        before = mx[0:1]
        top = jnp.maximum(before, jnp.max(raw, axis=0, keepdims=True))
        fade = jnp.exp2((before - top) * SCALE2)
        p = jnp.exp2((raw - top) * SCALE2)
        mx[0:1] = top
        tot[0:1] = tot[0:1] * fade + jnp.sum(p, axis=0, keepdims=True)
        dsum[0:1] = dsum[0:1] * fade + jnp.sum(p * grad_probs, axis=0, keepdims=True)

    def side(kind):
        return x + kind - 2 * x * kind

    def at(way, far):
        return lax.rem(z + Z - far, Z) if way == 0 else lax.rem(z + far, Z)

    def sib_number(way, e):
        return 2 + 6 * way + e

    def pass_on(e):
        far, kind = lax.div(e, 2) + 1, lax.rem(e, 2)
        for p in range(2):
            for way in range(2):
                s = dev(side(kind), at(way, far), c)
                arrive(s, p)
                if way + p == 1:
                    z_copy(way, s, e + 2, p).start()
                else:

                    @pl.when(far <= 2)
                    def _():
                        z_copy(way, s, e + 2, p).start()

                sib_copy(s, sib_number(way, e), p).start()

    def score_own(e):
        far, kind = lax.div(e, 2) + 1, lax.rem(e, 2)
        for way in range(2):
            scores(dev(side(kind), at(way, far), c))

    def score_sibling(e):
        far, kind = lax.div(e, 2) + 1, lax.rem(e, 2)
        for way in range(2):
            s = dev(side(kind), at(way, far), 1 - c)
            arrive(s, 0)
            arrive(s, 1)
            scores(s)

    for p in range(2):
        arrive(partner, p)
        z_copy(0, partner, 1, p).start()
        z_copy(1, partner, 1, p).start()
        sib_copy(partner, 1, p).start()
    pass_on(jnp.int32(0))
    for n in range(2):
        loads[7 + n].wait()
        q_copy(n).wait_recv()
    both = jnp.concatenate([key_positions(dev(0, z, c)), key_positions(dev(1, z, c))], axis=0)
    qpos[...] = both.T[0:8]

    def near(kind, carry):
        scores(dev(kind, z, c))
        return carry

    def near_sibling(kind, carry):
        s = dev(side(kind), z, 1 - c)
        arrive(s, 0)
        arrive(s, 1)
        scores(s)
        return carry

    lax.fori_loop(0, 2, near, 0)
    lax.fori_loop(0, 2, near_sibling, 0)

    def gather_step(e, carry):
        pass_on(e)
        score_own(e - 1)
        score_sibling(e - 1)
        return carry

    lax.fori_loop(1, 6, gather_step, 0)

    def far_pass(kind):
        for p in (1, 0):
            s = dev(side(kind), at(0, 4), c)
            arrive(s, p)
            sib_copy(s, 14 + kind, p).start()

    def far_own(kind, carry):
        scores(dev(side(kind), at(0, 4), c))
        return carry

    def far_sibling(kind, carry):
        s = dev(side(kind), at(0, 4), 1 - c)
        arrive(s, 0)
        arrive(s, 1)
        scores(s)
        return carry

    far_pass(0)
    score_own(jnp.int32(5))
    score_sibling(jnp.int32(5))
    far_pass(1)
    lax.fori_loop(0, 2, far_own, 0)
    lax.fori_loop(0, 2, far_sibling, 0)

    total = tot[0:1]
    mx[0:1] = mx[0:1] * SCALE2 + jnp.log2(total)
    dsum[0:1] = dsum[0:1] / total

    def grads(s):
        p = jnp.exp2(st[s] * SCALE2 - mx[0:1])
        grad_scores = (p * (dpt[s] - dsum[0:1])).astype(BF16)
        dv = jnp.dot(p.astype(BF16), gf[...], preferred_element_type=F32)
        dk = jnp.dot(grad_scores, qf[...], preferred_element_type=F32) * SCALE
        dqt[...] += lax.dot_general(kvg[s, keys], grad_scores, TN, preferred_element_type=F32)
        return dv, dk

    def g_copy(n):
        return push(sibs.at[n], sibr.at[n], g_send.at[n], g_recv.at[n], sibling)

    def r_copy(way, h, p):
        return push(snd.at[way, h, p], rcv.at[way, h, p], r_send.at[way, h, p], r_recv.at[way, h, p], (up, down)[way])

    def for_sibling(s, n):
        for p, term in enumerate(grads(s)):
            sibs[n, p] = term.astype(BF16)
        g_copy(n).start()

    def for_own(s, way):
        for p, term in enumerate(grads(s)):
            part[way, p] = term

    def farthest(h, carry):
        s = side(1 - h)
        for_sibling(dev(s, at(1, 4), 1 - c), h)
        for_own(dev(s, at(1, 4), c), 0)
        g_copy(h).wait_recv()
        for way in range(2):
            p = 1 - way
            snd[way, h, p] = (part[0, p] + sibr[h, p].astype(F32)).astype(BF16)
            r_copy(way, h, p).start()
        return carry

    lax.fori_loop(0, 2, farthest, 0)

    def reduce_step(h, carry):
        far = 4 - lax.div(h, 2)
        xx = side(1 - lax.rem(h, 2))
        n = 2 * h - 2
        for way in range(2):
            for_sibling(dev(xx, at(1 - way, far), 1 - c), n + way)
        for way in range(2):
            for_own(dev(xx, at(1 - way, far), c), way)
        for way in range(2):
            g_copy(n + way).wait_recv()
        for turn in range(2):
            for way in range(2):
                p = turn if way == 0 else 1 - turn
                here = part[way, p] + sibr[n + way, p].astype(F32)
                if turn == 0:

                    @pl.when(h >= 4)
                    def _():
                        r_copy(way, h - 2, p).wait_recv()
                        snd[way, h, p] = (here + rcv[way, h - 2, p].astype(F32)).astype(BF16)

                    @pl.when(h < 4)
                    def _():
                        snd[way, h, p] = here.astype(BF16)

                else:
                    r_copy(way, h - 2, p).wait_recv()
                    snd[way, h, p] = (here + rcv[way, h - 2, p].astype(F32)).astype(BF16)
                r_copy(way, h, p).start()
        return carry

    lax.fori_loop(2, 8, reduce_step, 0)

    def home_sibling(h, carry):
        for_sibling(dev(side(1 - h), z, 1 - c), 14 + h)
        return carry

    def home(h, carry):
        for_own(dev(side(1 - h), z, c), h)
        return carry

    lax.fori_loop(0, 2, home_sibling, 0)
    lax.fori_loop(0, 2, home, 0)

    grad_query = dqt[...].T * SCALE
    few = rows // heads
    for n in range(2 * heads):
        dqs[n] = grad_query[n * few : (n + 1) * few].astype(BF16)
    column = hd * 2 + x

    def d_copy(r):
        xx, gg = peer(r)
        n = xx * heads + gg
        return push(dqs.at[n], dqr.at[column], d_send.at[n], d_recv.at[column], dev(xx, z, c), gg)

    def d_wait(r):
        xx, gg = peer(r)
        source = gg * 2 + xx
        return push(dqs.at[0], dqr.at[source], d_send.at[0], d_recv.at[source], dev(xx, z, c), gg)

    for r in range(1, 2 * heads):
        d_copy(r).start()
    dqr[column] = dqs[flat]
    for h in range(2):
        g_copy(14 + h).wait_recv()

    def final(h, p):
        for way in range(2):
            r_copy(way, 6 + h, p).wait_recv()
        terms = part[h, p] + sibr[14 + h, p].astype(F32)
        return (terms + rcv[0, 6 + h, p].astype(F32) + rcv[1, 6 + h, p].astype(F32)).astype(BF16)

    def xr_copy(p):
        return push(xs.at[p], xr.at[p], xr_send.at[p], xr_recv.at[p], across)

    outs = (dv_ref, dk_ref)
    for p in range(2):
        xs[p] = final(0, p)
        xr_copy(p).start()
    for r in range(1, 2 * heads):
        d_wait(r).wait_recv()
    for n in range(2 * heads):
        dq_ref[:, n * 128 : (n + 1) * 128] = dqr[n]
    for p in range(2):
        outs[p][:, pl.ds(mine, 128)] = final(1, p)

    for way in range(2):
        for p in range(2):
            z_copy(way, me, 0, p).wait_send()
            z_copy(way, partner, 1, p).wait_send()

    def drain_gather(e, carry):
        for p in range(2):
            for way in range(2):
                if way + p == 1:
                    z_copy(way, me, e + 2, p).wait_send()
                else:

                    @pl.when(e < 4)
                    def _():
                        z_copy(way, me, e + 2, p).wait_send()

                r_copy(way, e + 2, p).wait_send()
        return carry

    lax.fori_loop(0, 6, drain_gather, 0)

    def drain_sibling(n, carry):
        for p in range(2):
            sib_copy(me, n, p).wait_send()
        g_copy(n).wait_send()
        return carry

    lax.fori_loop(0, 16, drain_sibling, 0)
    for h in range(2):
        r_copy(0, h, 1).wait_send()
        r_copy(1, h, 0).wait_send()
        x_copy(h).wait_send()
        q_copy(h).wait_send()
    for r in range(1, 2 * heads):
        d_copy(r).wait_send()
    for p in range(2):
        xr_copy(p).wait_recv()
        outs[p][:, pl.ds(other, 128)] = xr[p]
        xr_copy(p).wait_send()


def local(query_rows, key_rows, value_rows, grad_output, positions):
    rows, width = query_rows.shape
    heads = lax.axis_size("head")
    members = lax.axis_size("seq")
    vmem = pl.BlockSpec(memory_space=pltpu.VMEM)
    dma, tall = pltpu.SemaphoreType.DMA, 2 * rows + 16
    few = rows // heads
    return pl.pallas_call(
        kernel,
        out_shape=(
            pltpu.VMEM((few, heads * width), BF16),
            pltpu.VMEM((rows, width), BF16),
            pltpu.VMEM((rows, width), BF16),
        ),
        in_specs=[pl.BlockSpec(memory_space=pl.ANY)] * 5,
        out_specs=(vmem,) * 3,
        scratch_shapes=[
            pltpu.VMEM((members, tall, 128), BF16),
            pltpu.VMEM((tall, 128), BF16),
            pltpu.VMEM((2, rows, 128), BF16),
            pltpu.VMEM((2 * rows, 128), BF16),
            pltpu.VMEM((2 * rows, 128), BF16),
            pltpu.VMEM((1, rows), jnp.int32),
            pltpu.VMEM((16, 128), F32),
            pltpu.VMEM((members, rows, 2 * rows), F32),
            pltpu.VMEM((members, rows, 2 * rows), F32),
            pltpu.VMEM((8, 2 * rows), F32),
            pltpu.VMEM((8, 2 * rows), F32),
            pltpu.VMEM((8, 2 * rows), F32),
            pltpu.VMEM((8, 2 * rows), F32),
            pltpu.VMEM((128, 2 * rows), F32),
            pltpu.VMEM((16, 2, rows, 128), BF16),
            pltpu.VMEM((16, 2, rows, 128), BF16),
            pltpu.VMEM((2, 2, rows, 128), F32),
            pltpu.VMEM((2, 8, 2, rows, 128), BF16),
            pltpu.VMEM((2, 8, 2, rows, 128), BF16),
            pltpu.VMEM((2, rows, 128), BF16),
            pltpu.VMEM((2, rows, 128), BF16),
            pltpu.VMEM((2 * heads, few, 128), BF16),
            pltpu.VMEM((2 * heads, few, 128), BF16),
            dma((9,)),
            dma((members, 2)),
            dma((2, 8, 2)),
            dma((16, 2)),
            dma((4,)),
            dma((2,)),
            dma((16,)),
            dma((16,)),
            dma((2, 8, 2)),
            dma((2, 8, 2)),
            dma((2,)),
            dma((2,)),
            dma((2 * heads,)),
            dma((2 * heads,)),
        ],
        compiler_params=pltpu.CompilerParams(
            collective_id=0, has_side_effects=True, vmem_limit_bytes=60 * 1024 * 1024
        ),
    )(query_rows, key_rows, value_rows, grad_output, positions.reshape(1, rows))


def solution(mesh):
    placed = (P("seq", "head"), P("seq", "head"), P("seq", "head"), P("seq", "head"), P("seq"))
    return jax.shard_map(
        local,
        mesh=mesh,
        in_specs=placed,
        out_specs=(P(("seq", "head"), None), P("seq", "head"), P("seq", "head")),
        check_vma=False,
    )
```

time: 65.5 us -> 58.9 us (0.90)
  Pallas kernels: 60.2 us -> 56.2 us
  other arithmetic: 1.3 us -> 0 us
  local copies, waits for them, and re-layouts: 3.15 us -> 1.92 us
    pallas_call x1, Pallas kernels: 60.2 us -> 56.2 us  [local(): pl.pallas_call(kernel, out_shape=(pltpu.VMEM((few, heads * width), BF16),...]
    concatenate x2 -> x0, other arithmetic: 1.3 us -> none  [local(): jnp.concatenate([padded // 64, padded % 64]).astype(BF16).reshape(4, 128)]
    unnamed x7 -> x3, local copies, waits for them, and re-layouts: 3.15 us -> 1.92 us
where the time goes in v2:
time: 58.9 us; the launch traced here: 58.8 us
  Pallas kernels  56.2 us (95%)
  local copies, waits for them, and re-layouts  1.92 us (3%)
  between operations  0.64 us (1%)
    pallas_call x1, Pallas kernels, local(): pl.pallas_call(kernel, out_shape=(pltpu.VMEM((few, heads * width), BF16),...  56.2 us
    unnamed x3, local copies, waits for them, and re-layouts  1.92 us

profile of v2, /device:TPU:1, one launch (start us, length us, event | category | flops | bytes accessed | tf_op | source)
XLA Modules:
  0.0 58.8 jit_solution(14769934751579358586)
XLA Ops:
  0.6 56.2 %shard_map.76 = (bf16[24,2048]{1,0:T(8,128)(2,1)S(1)}, bf16[192,256]{1,0:T(8,128)(2,1)S(1)}, bf16[192,256]{1,0:T(8,128)(2,1)S(1)}) custom-call(bf16[192,256]{1,0:T(8,128)(2,1)} %q_ref.1, bf16[192,256]{1,0:T(8,128)(2,1)} %k_ref.1, bf16[192,256]{1,0:T(8,128)(2,1)} %v_ref.1, bf16[192,256]{1,0:T(8,128)(2,1)} %g_ref.1, s32[1,192]{1,0:T(1,128)} %bitcast.1), custom_call_target="tpu_custom_call" | custom-call | tf_op jit(solution)/shard_map/pallas_call | solution.py:419
  56.9 0.6 %copy.11 = bf16[24,2048]{1,0:T(8,128)(2,1)} copy(bf16[24,2048]{1,0:T(8,128)(2,1)S(1)} %get-tuple-element.3) | data formatting | bytes 196608
  57.5 0.6 %copy.12 = bf16[192,256]{1,0:T(8,128)(2,1)} copy(bf16[192,256]{1,0:T(8,128)(2,1)S(1)} %get-tuple-element.4) | data formatting | bytes 196608
  58.2 0.6 %copy.13 = bf16[192,256]{1,0:T(8,128)(2,1)} copy(bf16[192,256]{1,0:T(8,128)(2,1)S(1)} %get-tuple-element.5) | data formatting | bytes 196608

commit v3 on v2

--- a/solution.py
+++ b/solution.py
@@ -23,7 +23,7 @@
     kvg, xkv, xq, qf, gf, posr, posb, st, dpt, qpos, mx, tot, dsum, dqt,
     sibs, sibr, part, snd, rcv, xs, xr, dqs, dqr,
     l_sem, in_recv, z_send, sib_send, x_send, q_recv, g_send, g_recv,
-    r_send, r_recv, xr_send, xr_recv, d_send, d_recv,
+    r_send, r_recv, xr_send, xr_recv, d_send, d_recv, near_sem, go_sem, far_sem,
 ):
     rows = q_ref.shape[0]
     me, hd = lax.axis_index("seq"), lax.axis_index("head")
@@ -72,11 +72,18 @@
         return lax.div(there, heads), lax.rem(there, heads)
 
     barrier = pltpu.get_barrier_semaphore()
-    for seq in (up, down, sibling):
-        pl.semaphore_signal(barrier, inc=1, device_id={"seq": seq, "head": hd}, device_id_type=MESH)
-    for r in range(1, 2 * heads):
-        xx, gg = peer(r)
-        pl.semaphore_signal(barrier, inc=1, device_id={"seq": dev(xx, z, c), "head": gg}, device_id_type=MESH)
+
+    def signal(sem, seq, head=hd):
+        pl.semaphore_signal(sem, inc=1, device_id={"seq": seq, "head": head}, device_id_type=MESH)
+
+    @pl.when(c == 1)
+    def _():
+        for seq in (up, down, across):
+            signal(barrier, seq)
+
+    @pl.when(c == 0)
+    def _():
+        signal(barrier, sibling)
 
     mx[...] = jnp.full(mx.shape, FAR, F32)
     tot[...] = jnp.zeros(tot.shape, F32)
@@ -94,7 +101,15 @@
     kvg[me, tail] = posb[...].astype(BF16)
     xkv[tail] = posb[...].astype(BF16)
 
-    pl.semaphore_wait(barrier, 3 + 2 * heads - 1)
+    @pl.when(c == 1)
+    def _():
+        pl.semaphore_wait(barrier, 4)
+        for seq in (up, down, across):
+            signal(near_sem, seq)
+
+    @pl.when(c == 0)
+    def _():
+        pl.semaphore_wait(go_sem, 1)
 
     def z_copy(way, s, n, p):
         return push(kvg.at[s, cut[p]], kvg.at[s, cut[p]], z_send.at[way, n, p], in_recv.at[s, p], (up, down)[way])
@@ -118,6 +133,17 @@
     for n in range(2):
         loads[5 + n].wait()
         q_copy(n).start()
+
+    @pl.when(c == 1)
+    def _():
+        pl.semaphore_wait(near_sem, 3)
+        signal(go_sem, sibling)
+
+    @pl.when(c == 0)
+    def _():
+        for xx in range(2):
+            for r in range(1, heads):
+                signal(barrier, dev(xx, z, c), lax.rem(hd + r, heads))
 
     def arrive(s, p):
         sib_copy(s, 0, p).wait_recv()
@@ -265,66 +291,76 @@
             sibs[n, p] = term.astype(BF16)
         g_copy(n).start()
 
-    def for_own(s, way):
+    def for_own(s, h, way):
         for p, term in enumerate(grads(s)):
-            part[way, p] = term
+            part[h, way, p] = term
 
     def farthest(h, carry):
         s = side(1 - h)
         for_sibling(dev(s, at(1, 4), 1 - c), h)
-        for_own(dev(s, at(1, 4), c), 0)
+        for_own(dev(s, at(1, 4), c), h, 0)
         g_copy(h).wait_recv()
         for way in range(2):
             p = 1 - way
-            snd[way, h, p] = (part[0, p] + sibr[h, p].astype(F32)).astype(BF16)
+            snd[way, h, p] = (part[h, 0, p] + sibr[h, p].astype(F32)).astype(BF16)
             r_copy(way, h, p).start()
         return carry
 
     lax.fori_loop(0, 2, farthest, 0)
 
+    def step_terms(h):
+        far = 4 - lax.div(h, 2)
+        for way in range(2):
+            xx = side(jnp.where(h == 8, 1 - way, 1 - lax.rem(h, 2)))
+            for_sibling(dev(xx, at(1 - way, far), 1 - c), 2 * h - 2 + way)
+        for way in range(2):
+            xx = side(jnp.where(h == 8, 1 - way, 1 - lax.rem(h, 2)))
+            for_own(dev(xx, at(1 - way, far), c), h, way)
+
+    def here(h, way, p):
+        return part[h, way, p] + sibr[2 * h - 2 + way, p].astype(F32)
+
+    def send_first(h):
+        for way in range(2):
+            g_copy(2 * h - 2 + way).wait_recv()
+            snd[way, h, way] = here(h, way, way).astype(BF16)
+            r_copy(way, h, way).start()
+
+    def send_summed(h, turn):
+        for way in range(2):
+            p = turn if way == 0 else 1 - turn
+            r_copy(way, h - 2, p).wait_recv()
+            snd[way, h, p] = (here(h, way, p) + rcv[way, h - 2, p].astype(F32)).astype(BF16)
+            r_copy(way, h, p).start()
+
+    def send_both(h):
+        for way in range(2):
+            g_copy(2 * h - 2 + way).wait_recv()
+        send_summed(h, 0)
+        send_summed(h, 1)
+
+    def first_step(h, carry):
+        step_terms(h)
+        send_first(h)
+        return carry
+
+    lax.fori_loop(2, 4, first_step, 0)
+
     def reduce_step(h, carry):
-        far = 4 - lax.div(h, 2)
-        xx = side(1 - lax.rem(h, 2))
-        n = 2 * h - 2
-        for way in range(2):
-            for_sibling(dev(xx, at(1 - way, far), 1 - c), n + way)
-        for way in range(2):
-            for_own(dev(xx, at(1 - way, far), c), way)
-        for way in range(2):
-            g_copy(n + way).wait_recv()
-        for turn in range(2):
-            for way in range(2):
-                p = turn if way == 0 else 1 - turn
-                here = part[way, p] + sibr[n + way, p].astype(F32)
-                if turn == 0:
-
-                    @pl.when(h >= 4)
-                    def _():
-                        r_copy(way, h - 2, p).wait_recv()
-                        snd[way, h, p] = (here + rcv[way, h - 2, p].astype(F32)).astype(BF16)
-
-                    @pl.when(h < 4)
-                    def _():
-                        snd[way, h, p] = here.astype(BF16)
-
-                else:
-                    r_copy(way, h - 2, p).wait_recv()
-                    snd[way, h, p] = (here + rcv[way, h - 2, p].astype(F32)).astype(BF16)
-                r_copy(way, h, p).start()
-        return carry
-
-    lax.fori_loop(2, 8, reduce_step, 0)
-
-    def home_sibling(h, carry):
-        for_sibling(dev(side(1 - h), z, 1 - c), 14 + h)
-        return carry
-
-    def home(h, carry):
-        for_own(dev(side(1 - h), z, c), h)
-        return carry
-
-    lax.fori_loop(0, 2, home_sibling, 0)
-    lax.fori_loop(0, 2, home, 0)
+        step_terms(h)
+
+        @pl.when(h == 4)
+        def _():
+            send_summed(jnp.int32(2), 1)
+            send_summed(jnp.int32(3), 1)
+
+        @pl.when(jnp.logical_and(h > 4, h < 8))
+        def _():
+            send_both(h - 1)
+
+        return carry
+
+    lax.fori_loop(4, 9, reduce_step, 0)
 
     grad_query = dqt[...].T * SCALE
     few = rows // heads
@@ -342,16 +378,26 @@
         source = gg * 2 + xx
         return push(dqs.at[0], dqr.at[source], d_send.at[0], d_recv.at[source], dev(xx, z, c), gg)
 
+    @pl.when(c == 0)
+    def _():
+        pl.semaphore_wait(barrier, 2 * heads - 2)
+        signal(far_sem, sibling)
+
+    @pl.when(c == 1)
+    def _():
+        pl.semaphore_wait(far_sem, 1)
+
     for r in range(1, 2 * heads):
         d_copy(r).start()
     dqr[column] = dqs[flat]
+    send_both(jnp.int32(7))
     for h in range(2):
         g_copy(14 + h).wait_recv()
 
     def final(h, p):
         for way in range(2):
             r_copy(way, 6 + h, p).wait_recv()
-        terms = part[h, p] + sibr[14 + h, p].astype(F32)
+        terms = part[8, h, p] + sibr[14 + h, p].astype(F32)
         return (terms + rcv[0, 6 + h, p].astype(F32) + rcv[1, 6 + h, p].astype(F32)).astype(BF16)
 
     def xr_copy(p):
@@ -361,12 +407,12 @@
     for p in range(2):
         xs[p] = final(0, p)
         xr_copy(p).start()
+    for p in range(2):
+        outs[p][:, pl.ds(mine, 128)] = final(1, p)
     for r in range(1, 2 * heads):
         d_wait(r).wait_recv()
     for n in range(2 * heads):
         dq_ref[:, n * 128 : (n + 1) * 128] = dqr[n]
-    for p in range(2):
-        outs[p][:, pl.ds(mine, 128)] = final(1, p)
 
     for way in range(2):
         for p in range(2):
@@ -442,7 +488,7 @@
             pltpu.VMEM((128, 2 * rows), F32),
             pltpu.VMEM((16, 2, rows, 128), BF16),
             pltpu.VMEM((16, 2, rows, 128), BF16),
-            pltpu.VMEM((2, 2, rows, 128), F32),
+            pltpu.VMEM((9, 2, 2, rows, 128), F32),
             pltpu.VMEM((2, 8, 2, rows, 128), BF16),
             pltpu.VMEM((2, 8, 2, rows, 128), BF16),
             pltpu.VMEM((2, rows, 128), BF16),
@@ -463,6 +509,9 @@
             dma((2,)),
             dma((2 * heads,)),
             dma((2 * heads,)),
+            pltpu.SemaphoreType.REGULAR,
+            pltpu.SemaphoreType.REGULAR,
+            pltpu.SemaphoreType.REGULAR,
         ],
         compiler_params=pltpu.CompilerParams(
             collective_id=0, has_side_effects=True, vmem_limit_bytes=60 * 1024 * 1024

time: 58.9 us -> 56.4 us (0.958)
  Pallas kernels: 56.2 us -> 53.7 us
    pallas_call x1, Pallas kernels: 56.2 us -> 53.7 us  [local(): pl.pallas_call(kernel, out_shape=(pltpu.VMEM((few, heads * width), BF16),...]
where the time goes in v3:
time: 56.4 us; the launch traced here: 56.2 us
  Pallas kernels  53.7 us (95%)
  local copies, waits for them, and re-layouts  1.92 us (3%)
  between operations  0.64 us (1%)
    pallas_call x1, Pallas kernels, local(): pl.pallas_call(kernel, out_shape=(pltpu.VMEM((few, heads * width), BF16),...  53.7 us
    unnamed x3, local copies, waits for them, and re-layouts  1.92 us

profile of v3, /device:TPU:1, one launch (start us, length us, event | category | flops | bytes accessed | tf_op | source)
XLA Modules:
  0.0 56.2 jit_solution(4666078345483927659)
XLA Ops:
  0.6 53.7 %shard_map.76 = (bf16[24,2048]{1,0:T(8,128)(2,1)S(1)}, bf16[192,256]{1,0:T(8,128)(2,1)S(1)}, bf16[192,256]{1,0:T(8,128)(2,1)S(1)}) custom-call(bf16[192,256]{1,0:T(8,128)(2,1)} %q_ref.1, bf16[192,256]{1,0:T(8,128)(2,1)} %k_ref.1, bf16[192,256]{1,0:T(8,128)(2,1)} %v_ref.1, bf16[192,256]{1,0:T(8,128)(2,1)} %g_ref.1, s32[1,192]{1,0:T(1,128)} %bitcast.1), custom_call_target="tpu_custom_call" | custom-call | tf_op jit(solution)/shard_map/pallas_call | solution.py:465
  54.3 0.6 %copy.11 = bf16[24,2048]{1,0:T(8,128)(2,1)} copy(bf16[24,2048]{1,0:T(8,128)(2,1)S(1)} %get-tuple-element.3) | data formatting | bytes 196608
  55.0 0.6 %copy.12 = bf16[192,256]{1,0:T(8,128)(2,1)} copy(bf16[192,256]{1,0:T(8,128)(2,1)S(1)} %get-tuple-element.4) | data formatting | bytes 196608
  55.6 0.6 %copy.13 = bf16[192,256]{1,0:T(8,128)(2,1)} copy(bf16[192,256]{1,0:T(8,128)(2,1)S(1)} %get-tuple-element.5) | data formatting | bytes 196608

commit v4 on v3

--- a/solution.py
+++ b/solution.py
@@ -13,6 +13,7 @@
 SCALE2 = SCALE * math.log2(math.e)
 FAR = -1e30
 Z = 8
+PIECES = 4
 F32, BF16 = jnp.float32, jnp.bfloat16
 NT = (((1,), (1,)), ((), ()))
 TN = (((0,), (0,)), ((), ()))
@@ -43,8 +44,9 @@
             device_id={"seq": seq, "head": head}, device_id_type=MESH,
         )
 
-    vals, keys, tail = pl.ds(0, rows), pl.ds(rows, rows), pl.ds(2 * rows, 16)
-    cut = (pl.ds(0, rows), pl.ds(rows, rows + 16))
+    vals, keys, tail = pl.ds(0, rows), pl.ds(rows, rows), pl.ds(2 * rows, 8)
+    some = rows // 2
+    cut = (pl.ds(0, some), pl.ds(some, some), pl.ds(rows, some), pl.ds(rows + some, some + 8))
 
     mine, other = pl.multiple_of(x * 128, 128), pl.multiple_of((1 - x) * 128, 128)
     held = pl.ds(pl.multiple_of(x * rows, rows), rows)
@@ -121,15 +123,17 @@
         return push(xkv.at[cut[p]], kvg.at[me, cut[p]], x_send.at[p], in_recv.at[me, p], across)
 
     def q_copy(n):
-        return push(xq.at[n], (qf, gf)[n].at[held], x_send.at[2 + n], q_recv.at[n], across)
-
-    for p in range(2):
-        loads[1 + 2 * p].wait()
-        z_copy(0, me, 0, p).start()
-        z_copy(1, me, 0, p).start()
-        loads[2 + 2 * p].wait()
-        x_copy(p).start()
-        sib_copy(me, 0, p).start()
+        return push(xq.at[n], (qf, gf)[n].at[held], x_send.at[4 + n], q_recv.at[n], across)
+
+    for half in range(2):
+        loads[1 + 2 * half].wait()
+        loads[2 + 2 * half].wait()
+        for p in (2 * half, 2 * half + 1):
+            z_copy(0, me, 0, p).start()
+            z_copy(1, me, 0, p).start()
+            x_copy(p).start()
+        for p in (2 * half, 2 * half + 1):
+            sib_copy(me, 0, p).start()
     for n in range(2):
         loads[5 + n].wait()
         q_copy(n).start()
@@ -149,7 +153,7 @@
         sib_copy(s, 0, p).wait_recv()
 
     def key_positions(s):
-        block = kvg[s, 2 * rows : 2 * rows + 16].astype(F32)
+        block = kvg[s, 2 * rows : 2 * rows + 8].astype(F32)
         first = block[0:1] * 64.0 + block[2:3]
         rest = block[1:2] * 64.0 + block[3:4]
         return jnp.concatenate(
@@ -183,11 +187,11 @@
 
     def pass_on(e):
         far, kind = lax.div(e, 2) + 1, lax.rem(e, 2)
-        for p in range(2):
+        for p in range(PIECES):
             for way in range(2):
                 s = dev(side(kind), at(way, far), c)
                 arrive(s, p)
-                if way + p == 1:
+                if p // 2 != way:
                     z_copy(way, s, e + 2, p).start()
                 else:
 
@@ -197,6 +201,10 @@
 
                 sib_copy(s, sib_number(way, e), p).start()
 
+    def arrive_whole(s):
+        for p in range(PIECES):
+            arrive(s, p)
+
     def score_own(e):
         far, kind = lax.div(e, 2) + 1, lax.rem(e, 2)
         for way in range(2):
@@ -206,11 +214,10 @@
         far, kind = lax.div(e, 2) + 1, lax.rem(e, 2)
         for way in range(2):
             s = dev(side(kind), at(way, far), 1 - c)
-            arrive(s, 0)
-            arrive(s, 1)
+            arrive_whole(s)
             scores(s)
 
-    for p in range(2):
+    for p in range(PIECES):
         arrive(partner, p)
         z_copy(0, partner, 1, p).start()
         z_copy(1, partner, 1, p).start()
@@ -228,8 +235,7 @@
 
     def near_sibling(kind, carry):
         s = dev(side(kind), z, 1 - c)
-        arrive(s, 0)
-        arrive(s, 1)
+        arrive_whole(s)
         scores(s)
         return carry
 
@@ -245,7 +251,7 @@
     lax.fori_loop(1, 6, gather_step, 0)
 
     def far_pass(kind):
-        for p in (1, 0):
+        for p in (2, 0, 3, 1):
             s = dev(side(kind), at(0, 4), c)
             arrive(s, p)
             sib_copy(s, 14 + kind, p).start()
@@ -256,8 +262,7 @@
 
     def far_sibling(kind, carry):
         s = dev(side(kind), at(0, 4), 1 - c)
-        arrive(s, 0)
-        arrive(s, 1)
+        arrive_whole(s)
         scores(s)
         return carry
 
@@ -295,10 +300,12 @@
         for p, term in enumerate(grads(s)):
             part[h, way, p] = term
 
+    def farthest_sibling(h, carry):
+        for_sibling(dev(side(1 - h), at(1, 4), 1 - c), h)
+        return carry
+
     def farthest(h, carry):
-        s = side(1 - h)
-        for_sibling(dev(s, at(1, 4), 1 - c), h)
-        for_own(dev(s, at(1, 4), c), h, 0)
+        for_own(dev(side(1 - h), at(1, 4), c), h, 0)
         g_copy(h).wait_recv()
         for way in range(2):
             p = 1 - way
@@ -306,6 +313,7 @@
             r_copy(way, h, p).start()
         return carry
 
+    lax.fori_loop(0, 2, farthest_sibling, 0)
     lax.fori_loop(0, 2, farthest, 0)
 
     def step_terms(h):
@@ -415,14 +423,14 @@
         dq_ref[:, n * 128 : (n + 1) * 128] = dqr[n]
 
     for way in range(2):
-        for p in range(2):
+        for p in range(PIECES):
             z_copy(way, me, 0, p).wait_send()
             z_copy(way, partner, 1, p).wait_send()
 
     def drain_gather(e, carry):
-        for p in range(2):
-            for way in range(2):
-                if way + p == 1:
+        for way in range(2):
+            for p in range(PIECES):
+                if p // 2 != way:
                     z_copy(way, me, e + 2, p).wait_send()
                 else:
 
@@ -430,13 +438,14 @@
                     def _():
                         z_copy(way, me, e + 2, p).wait_send()
 
+            for p in range(2):
                 r_copy(way, e + 2, p).wait_send()
         return carry
 
     lax.fori_loop(0, 6, drain_gather, 0)
 
     def drain_sibling(n, carry):
-        for p in range(2):
+        for p in range(PIECES):
             sib_copy(me, n, p).wait_send()
         g_copy(n).wait_send()
         return carry
@@ -446,6 +455,7 @@
         r_copy(0, h, 1).wait_send()
         r_copy(1, h, 0).wait_send()
         x_copy(h).wait_send()
+        x_copy(2 + h).wait_send()
         q_copy(h).wait_send()
     for r in range(1, 2 * heads):
         d_copy(r).wait_send()
@@ -455,14 +465,23 @@
         xr_copy(p).wait_send()
 
 
+def store(dq_ref, dk_ref, dv_ref, dq_out, dk_out, dv_out, sems):
+    pairs = ((dq_ref, dq_out), (dk_ref, dk_out), (dv_ref, dv_out))
+    copies = [pltpu.make_async_copy(src, dst, sems.at[n]) for n, (src, dst) in enumerate(pairs)]
+    for copy in copies:
+        copy.start()
+    for copy in copies:
+        copy.wait()
+
+
 def local(query_rows, key_rows, value_rows, grad_output, positions):
     rows, width = query_rows.shape
     heads = lax.axis_size("head")
     members = lax.axis_size("seq")
     vmem = pl.BlockSpec(memory_space=pltpu.VMEM)
-    dma, tall = pltpu.SemaphoreType.DMA, 2 * rows + 16
+    dma, tall = pltpu.SemaphoreType.DMA, 2 * rows + 8
     few = rows // heads
-    return pl.pallas_call(
+    held = pl.pallas_call(
         kernel,
         out_shape=(
             pltpu.VMEM((few, heads * width), BF16),
@@ -478,7 +497,7 @@
             pltpu.VMEM((2 * rows, 128), BF16),
             pltpu.VMEM((2 * rows, 128), BF16),
             pltpu.VMEM((1, rows), jnp.int32),
-            pltpu.VMEM((16, 128), F32),
+            pltpu.VMEM((8, 128), F32),
             pltpu.VMEM((members, rows, 2 * rows), F32),
             pltpu.VMEM((members, rows, 2 * rows), F32),
             pltpu.VMEM((8, 2 * rows), F32),
@@ -496,10 +515,10 @@
             pltpu.VMEM((2 * heads, few, 128), BF16),
             pltpu.VMEM((2 * heads, few, 128), BF16),
             dma((9,)),
-            dma((members, 2)),
-            dma((2, 8, 2)),
-            dma((16, 2)),
-            dma((4,)),
+            dma((members, PIECES)),
+            dma((2, 8, PIECES)),
+            dma((16, PIECES)),
+            dma((PIECES + 2,)),
             dma((2,)),
             dma((16,)),
             dma((16,)),
@@ -517,6 +536,14 @@
             collective_id=0, has_side_effects=True, vmem_limit_bytes=60 * 1024 * 1024
         ),
     )(query_rows, key_rows, value_rows, grad_output, positions.reshape(1, rows))
+    held = [pltpu.with_memory_space_constraint(h, pltpu.VMEM) for h in held]
+    return pl.pallas_call(
+        store,
+        out_shape=tuple(jax.ShapeDtypeStruct(h.shape, h.dtype) for h in held),
+        in_specs=[vmem] * 3,
+        out_specs=(pl.BlockSpec(memory_space=pl.ANY),) * 3,
+        scratch_shapes=[dma((3,))],
+    )(*held)
 
 
 def solution(mesh):

time: 56.4 us -> 55.2 us (0.979)
  local copies, waits for them, and re-layouts: 1.92 us -> 0 us
  Pallas kernels: 53.7 us -> 54.5 us
    unnamed x3 -> x0, local copies, waits for them, and re-layouts: 1.92 us -> none
    pallas_call x0 -> x1, Pallas kernels: none -> 0.73 us  [local(): pl.pallas_call(store, out_shape=tuple((jax.ShapeDtypeStruct(h.shape, h.dt...]
where the time goes in v4:
time: 55.2 us; the launch traced here: 55.1 us
  Pallas kernels  54.5 us (99%)
  between operations  0.64 us (1%)
    pallas_call x1, Pallas kernels, local(): pl.pallas_call(kernel, out_shape=(pltpu.VMEM((few, heads * width), BF16),...  53.7 us

profile of v4, /device:TPU:1, one launch (start us, length us, event | category | flops | bytes accessed | tf_op | source)
XLA Modules:
  0.0 55.1 jit_solution(3171476527198938298)
XLA Ops:
  0.6 53.7 %shard_map.76 = (bf16[24,2048]{1,0:T(8,128)(2,1)S(1)}, bf16[192,256]{1,0:T(8,128)(2,1)S(1)}, bf16[192,256]{1,0:T(8,128)(2,1)S(1)}) custom-call(bf16[192,256]{1,0:T(8,128)(2,1)} %q_ref.1, bf16[192,256]{1,0:T(8,128)(2,1)} %k_ref.1, bf16[192,256]{1,0:T(8,128)(2,1)} %v_ref.1, bf16[192,256]{1,0:T(8,128)(2,1)} %g_ref.1, s32[1,192]{1,0:T(1,128)} %bitcast.1), custom_call_target="tpu_custom_call" | custom-call | tf_op jit(solution)/shard_map/pallas_call | solution.py:484
  54.4 0.7 %shard_map.77 = (bf16[24,2048]{1,0:T(8,128)(2,1)}, bf16[192,256]{1,0:T(8,128)(2,1)}, bf16[192,256]{1,0:T(8,128)(2,1)}) custom-call(bf16[24,2048]{1,0:T(8,128)(2,1)S(1)} %get-tuple-element.6.dq_ref, bf16[192,256]{1,0:T(8,128)(2,1)S(1)} %get-tuple-element.7.dk_ref, bf16[192,256]{1,0:T(8,128)(2,1)S(1)} %get-tuple-element.8.dv_ref), custom_call_target="tpu_custom_call" | custom-call | tf_op jit(solution)/shard_map/pallas_call | solution.py:540

commit v5 on v4

--- a/solution.py
+++ b/solution.py
@@ -24,7 +24,7 @@
     kvg, xkv, xq, qf, gf, posr, posb, st, dpt, qpos, mx, tot, dsum, dqt,
     sibs, sibr, part, snd, rcv, xs, xr, dqs, dqr,
     l_sem, in_recv, z_send, sib_send, x_send, q_recv, g_send, g_recv,
-    r_send, r_recv, xr_send, xr_recv, d_send, d_recv, near_sem, go_sem, far_sem,
+    r_send, r_recv, xr_send, xr_recv, d_send, d_recv, go_sem, far_sem,
 ):
     rows = q_ref.shape[0]
     me, hd = lax.axis_index("seq"), lax.axis_index("head")
@@ -78,14 +78,12 @@
     def signal(sem, seq, head=hd):
         pl.semaphore_signal(sem, inc=1, device_id={"seq": seq, "head": head}, device_id_type=MESH)
 
-    @pl.when(c == 1)
-    def _():
-        for seq in (up, down, across):
+    near_by = (up, down, across, sibling)
+    for seq in near_by:
+
+        @pl.when(seq != 0)
+        def _():
             signal(barrier, seq)
-
-    @pl.when(c == 0)
-    def _():
-        signal(barrier, sibling)
 
     mx[...] = jnp.full(mx.shape, FAR, F32)
     tot[...] = jnp.zeros(tot.shape, F32)
@@ -103,15 +101,18 @@
     kvg[me, tail] = posb[...].astype(BF16)
     xkv[tail] = posb[...].astype(BF16)
 
-    @pl.when(c == 1)
+    @pl.when(me != 0)
     def _():
         pl.semaphore_wait(barrier, 4)
-        for seq in (up, down, across):
-            signal(near_sem, seq)
-
-    @pl.when(c == 0)
+        for seq in near_by:
+
+            @pl.when(seq == 0)
+            def _():
+                signal(go_sem, seq)
+
+    @pl.when(me == 0)
     def _():
-        pl.semaphore_wait(go_sem, 1)
+        pl.semaphore_wait(go_sem, 4)
 
     def z_copy(way, s, n, p):
         return push(kvg.at[s, cut[p]], kvg.at[s, cut[p]], z_send.at[way, n, p], in_recv.at[s, p], (up, down)[way])
@@ -137,17 +138,6 @@
     for n in range(2):
         loads[5 + n].wait()
         q_copy(n).start()
-
-    @pl.when(c == 1)
-    def _():
-        pl.semaphore_wait(near_sem, 3)
-        signal(go_sem, sibling)
-
-    @pl.when(c == 0)
-    def _():
-        for xx in range(2):
-            for r in range(1, heads):
-                signal(barrier, dev(xx, z, c), lax.rem(hd + r, heads))
 
     def arrive(s, p):
         sib_copy(s, 0, p).wait_recv()
@@ -273,6 +263,11 @@
     lax.fori_loop(0, 2, far_own, 0)
     lax.fori_loop(0, 2, far_sibling, 0)
 
+    @pl.when(me == 0)
+    def _():
+        for r in range(1, heads):
+            signal(barrier, me, lax.rem(hd + r, heads))
+
     total = tot[0:1]
     mx[0:1] = mx[0:1] * SCALE2 + jnp.log2(total)
     dsum[0:1] = dsum[0:1] / total
@@ -355,6 +350,16 @@
     lax.fori_loop(2, 4, first_step, 0)
 
     def reduce_step(h, carry):
+        @pl.when(jnp.logical_and(h == 6, me == 0))
+        def _():
+            pl.semaphore_wait(barrier, heads - 1)
+
+            def tell(n, carry):
+                signal(far_sem, n)
+                return carry
+
+            lax.fori_loop(1, lax.axis_size("seq"), tell, 0)
+
         step_terms(h)
 
         @pl.when(h == 4)
@@ -386,12 +391,7 @@
         source = gg * 2 + xx
         return push(dqs.at[0], dqr.at[source], d_send.at[0], d_recv.at[source], dev(xx, z, c), gg)
 
-    @pl.when(c == 0)
-    def _():
-        pl.semaphore_wait(barrier, 2 * heads - 2)
-        signal(far_sem, sibling)
-
-    @pl.when(c == 1)
+    @pl.when(me != 0)
     def _():
         pl.semaphore_wait(far_sem, 1)
 
@@ -530,7 +530,6 @@
             dma((2 * heads,)),
             pltpu.SemaphoreType.REGULAR,
             pltpu.SemaphoreType.REGULAR,
-            pltpu.SemaphoreType.REGULAR,
         ],
         compiler_params=pltpu.CompilerParams(
             collective_id=0, has_side_effects=True, vmem_limit_bytes=60 * 1024 * 1024

time: 55.2 us -> 54.3 us (0.984); the launches traced: 55.1 us -> 53.6 us
  Pallas kernels: 54.5 us -> 53 us
    pallas_call x1, Pallas kernels: 53.7 us -> 52.3 us  [local(): pl.pallas_call(kernel, out_shape=(pltpu.VMEM((few, heads * width), BF16),...]
where the time goes in v5:
time: 54.3 us; the launch traced here: 53.6 us
  Pallas kernels  53 us (98%)
  between operations  0.64 us (1%)
    pallas_call x1, Pallas kernels, local(): pl.pallas_call(kernel, out_shape=(pltpu.VMEM((few, heads * width), BF16),...  52.3 us

profile of v5, /device:TPU:1, one launch (start us, length us, event | category | flops | bytes accessed | tf_op | source)
XLA Modules:
  0.0 53.6 jit_solution(12605857154289745504)
XLA Ops:
  0.6 52.3 %shard_map.76 = (bf16[24,2048]{1,0:T(8,128)(2,1)S(1)}, bf16[192,256]{1,0:T(8,128)(2,1)S(1)}, bf16[192,256]{1,0:T(8,128)(2,1)S(1)}) custom-call(bf16[192,256]{1,0:T(8,128)(2,1)} %q_ref.1, bf16[192,256]{1,0:T(8,128)(2,1)} %k_ref.1, bf16[192,256]{1,0:T(8,128)(2,1)} %v_ref.1, bf16[192,256]{1,0:T(8,128)(2,1)} %g_ref.1, s32[1,192]{1,0:T(1,128)} %bitcast.1), custom_call_target="tpu_custom_call" | custom-call | tf_op jit(solution)/shard_map/pallas_call | solution.py:484
  52.9 0.7 %shard_map.77 = (bf16[24,2048]{1,0:T(8,128)(2,1)}, bf16[192,256]{1,0:T(8,128)(2,1)}, bf16[192,256]{1,0:T(8,128)(2,1)}) custom-call(bf16[24,2048]{1,0:T(8,128)(2,1)S(1)} %get-tuple-element.6.dq_ref, bf16[192,256]{1,0:T(8,128)(2,1)S(1)} %get-tuple-element.7.dk_ref, bf16[192,256]{1,0:T(8,128)(2,1)S(1)} %get-tuple-element.8.dv_ref), custom_call_target="tpu_custom_call" | custom-call | tf_op jit(solution)/shard_map/pallas_call | solution.py:539

commit v6 on v5

--- a/solution.py
+++ b/solution.py
@@ -350,7 +350,7 @@
     lax.fori_loop(2, 4, first_step, 0)
 
     def reduce_step(h, carry):
-        @pl.when(jnp.logical_and(h == 6, me == 0))
+        @pl.when(jnp.logical_and(h == 5, me == 0))
         def _():
             pl.semaphore_wait(barrier, heads - 1)
 

time: 54.3 us -> 54.3 us (level)
  no operation moved by 1% of the time
where the time goes in v6:
time: 54.3 us; the launch traced here: 53.6 us
  Pallas kernels  53 us (98%)
  between operations  0.64 us (1%)
    pallas_call x1, Pallas kernels, local(): pl.pallas_call(kernel, out_shape=(pltpu.VMEM((few, heads * width), BF16),...  52.3 us

profile of v6, /device:TPU:1, one launch (start us, length us, event | category | flops | bytes accessed | tf_op | source)
XLA Modules:
  0.0 53.6 jit_solution(14510560785589286359)
XLA Ops:
  0.6 52.3 %shard_map.76 = (bf16[24,2048]{1,0:T(8,128)(2,1)S(1)}, bf16[192,256]{1,0:T(8,128)(2,1)S(1)}, bf16[192,256]{1,0:T(8,128)(2,1)S(1)}) custom-call(bf16[192,256]{1,0:T(8,128)(2,1)} %q_ref.1, bf16[192,256]{1,0:T(8,128)(2,1)} %k_ref.1, bf16[192,256]{1,0:T(8,128)(2,1)} %v_ref.1, bf16[192,256]{1,0:T(8,128)(2,1)} %g_ref.1, s32[1,192]{1,0:T(1,128)} %bitcast.1), custom_call_target="tpu_custom_call" | custom-call | tf_op jit(solution)/shard_map/pallas_call | solution.py:484
  52.9 0.7 %shard_map.77 = (bf16[24,2048]{1,0:T(8,128)(2,1)}, bf16[192,256]{1,0:T(8,128)(2,1)}, bf16[192,256]{1,0:T(8,128)(2,1)}) custom-call(bf16[24,2048]{1,0:T(8,128)(2,1)S(1)} %get-tuple-element.6.dq_ref, bf16[192,256]{1,0:T(8,128)(2,1)S(1)} %get-tuple-element.7.dk_ref, bf16[192,256]{1,0:T(8,128)(2,1)S(1)} %get-tuple-element.8.dv_ref), custom_call_target="tpu_custom_call" | custom-call | tf_op jit(solution)/shard_map/pallas_call | solution.py:539

commit v7 on v5

--- a/solution.py
+++ b/solution.py
@@ -128,10 +128,11 @@
 
     for half in range(2):
         loads[1 + 2 * half].wait()
-        loads[2 + 2 * half].wait()
         for p in (2 * half, 2 * half + 1):
             z_copy(0, me, 0, p).start()
             z_copy(1, me, 0, p).start()
+        loads[2 + 2 * half].wait()
+        for p in (2 * half, 2 * half + 1):
             x_copy(p).start()
         for p in (2 * half, 2 * half + 1):
             sib_copy(me, 0, p).start()

time: 54.3 us -> 54.3 us (level)
  no operation moved by 1% of the time
where the time goes in v7:
time: 54.3 us; the launch traced here: 53.7 us
  Pallas kernels  53 us (98%)
  between operations  0.64 us (1%)
    pallas_call x1, Pallas kernels, local(): pl.pallas_call(kernel, out_shape=(pltpu.VMEM((few, heads * width), BF16),...  52.3 us

profile of v7, /device:TPU:1, one launch (start us, length us, event | category | flops | bytes accessed | tf_op | source)
XLA Modules:
  0.0 53.7 jit_solution(8677831605894650070)
XLA Ops:
  0.6 52.3 %shard_map.76 = (bf16[24,2048]{1,0:T(8,128)(2,1)S(1)}, bf16[192,256]{1,0:T(8,128)(2,1)S(1)}, bf16[192,256]{1,0:T(8,128)(2,1)S(1)}) custom-call(bf16[192,256]{1,0:T(8,128)(2,1)} %q_ref.1, bf16[192,256]{1,0:T(8,128)(2,1)} %k_ref.1, bf16[192,256]{1,0:T(8,128)(2,1)} %v_ref.1, bf16[192,256]{1,0:T(8,128)(2,1)} %g_ref.1, s32[1,192]{1,0:T(1,128)} %bitcast.1), custom_call_target="tpu_custom_call" | custom-call | tf_op jit(solution)/shard_map/pallas_call | solution.py:485
  52.9 0.7 %shard_map.77 = (bf16[24,2048]{1,0:T(8,128)(2,1)}, bf16[192,256]{1,0:T(8,128)(2,1)}, bf16[192,256]{1,0:T(8,128)(2,1)}) custom-call(bf16[24,2048]{1,0:T(8,128)(2,1)S(1)} %get-tuple-element.6.dq_ref, bf16[192,256]{1,0:T(8,128)(2,1)S(1)} %get-tuple-element.7.dk_ref, bf16[192,256]{1,0:T(8,128)(2,1)S(1)} %get-tuple-element.8.dv_ref), custom_call_target="tpu_custom_call" | custom-call | tf_op jit(solution)/shard_map/pallas_call | solution.py:540
